TPU v7x, 32 devices: a whole 2x2x4 slice. The times are simulated.
32 devices in a mesh: mesh: 8 (over y, x, core), harm: 4 (over z).
Axes of the slice: x: 2, y: 2, z: 4, core: 2. Of those that a mesh axis runs over, the one named last changes fastest.
Arguments:
- field_in: float32 [64, 40960], P('harm', 'mesh'), may hold values from -6 to 6
- faces: int32 [2, 8192], P(None, 'mesh'), may hold values from 0 to 5119, as said below
- connectivity: int32 [6, 32768], P(None, 'mesh'), may hold values from 0 to 7167
- curl_vectors: float32 [3, 6, 32768], P(None, None, 'mesh'), may hold values from -2.4 to 2.4
- operating_point: float32 [64, 3, 8, 4096], P(None, None, None, ('mesh', 'harm')), may hold values from -2.5 to 2.5
- material: int32 [8, 4096], P(None, ('mesh', 'harm')), may hold values from 0 to 3
- bh_knots: int32 [8], replicated, may hold values from 0 to 15
- curve_base: float32 [4], replicated, may hold values from 0.5 to 2
- curve_slopes: float32 [4, 8], replicated, may hold values from 0.02 to 0.2
Outputs:
- product: float32 [64, 40960], P('harm', 'mesh')
Inputs may be any that keep to these rules, and one draw needn't show every extreme that they name: `faces`: for each partition the 1024 lower face edges and the 1024 upper face edges are 2048 distinct local edge numbers. `connectivity`: numbers below 5120 are the partition's own edges, the next 1024 the ghost edges after the upper face list of the partition below, the last 1024 those after the lower face list of the partition above.
All inputs are finite; a program needn't handle non-finite values.
Results may differ from a plain program's by a relative error of at most 0.0003.
Values sent between devices are 32-bit elements; how exact they have to be, the bound alone decides.
No kernel may reach another device: no remote copies, remote signals or barrier semaphores. Data moves between devices by JAX's collectives and lax.ppermute only.
A program may use at most 128 MiB of HBM per device.

v0:
```python
import jax
import jax.numpy as jnp
from jax import lax
from jax.sharding import PartitionSpec as P

KNOT_STEP = 0.25
KNOT_WIDTH = 0.5


def with_halo(value, sides, width):
    for axis, dim in sides:
        count, length = (lax.axis_size(axis), value.shape[dim])
        up = [(i, (i + 1) % count) for i in range(count)]
        down = [(j, i) for i, j in up]
        last = lax.slice_in_dim(value, length - width, length, axis=dim)
        first = lax.slice_in_dim(value, 0, width, axis=dim)
        before = lax.ppermute(last, axis, up)
        after = lax.ppermute(first, axis, down)
        value = jnp.concatenate([before, value, after], axis=dim)
    return value


def dft_tables(length):
    sample_idx = jnp.arange(length, dtype=jnp.int32)
    coef_idx = jnp.arange(length, dtype=jnp.int32)
    half_len = length // 2
    harmonic = jnp.where(coef_idx < half_len, coef_idx, coef_idx - half_len + 1)
    harmonic = jnp.where(coef_idx == length - 1, half_len, harmonic)
    is_sine = (coef_idx >= half_len) & (coef_idx < length - 1)
    phase_int = harmonic[:, None] * sample_idx[None, :] % length
    angles = phase_int.astype(jnp.float32) * (2.0 * jnp.pi / length)
    basis_rows = jnp.where(is_sine[:, None], jnp.sin(angles), jnp.cos(angles))
    weight = jnp.where((coef_idx == 0) | (coef_idx == length - 1), 1.0 / length, 2.0 / length)
    return (basis_rows.T, basis_rows * weight[:, None].astype(jnp.float32))


def apply_tensor(flux_step, point, material, bh_knots, curve_base, curve_slopes):
    kind_ids = jnp.arange(curve_base.shape[0], dtype=jnp.int32).reshape(
        (-1,) + (1,) * material.ndim
    )
    one_hot = (material[None] == kind_ids).astype(jnp.float32)
    base_elem = jnp.einsum("a,a...->...", curve_base, one_hot, precision=lax.Precision.HIGHEST)
    slope_elem = jnp.einsum("ak,a...->k...", curve_slopes, one_hot, precision=lax.Precision.HIGHEST)
    flux_sq = jnp.sum(point * point, axis=1)
    knot_pos = bh_knots.astype(jnp.float32) * KNOT_STEP
    scaled = (flux_sq[None] - knot_pos.reshape((-1,) + (1,) * flux_sq.ndim)) / KNOT_WIDTH
    reluct = base_elem[None] + jnp.sum(slope_elem[:, None] * jax.nn.softplus(scaled), axis=0)
    slope_sum = jnp.sum(slope_elem[:, None] * jax.nn.sigmoid(scaled), axis=0) / KNOT_WIDTH
    projected = jnp.sum(point * flux_step, axis=1)
    return reluct[:, None] * flux_step + 2.0 * (slope_sum * projected)[:, None] * point


def per_device(
    field_in,
    faces,
    connectivity,
    curl_vectors,
    operating_point,
    material,
    bh_knots,
    curve_base,
    curve_slopes,
):
    coeffs = field_in.shape[0]
    own_edges = field_in.shape[1]
    face_len = faces.shape[1]
    elements = connectivity.shape[1]
    mesh_count = lax.axis_size("mesh")
    harm_count = lax.axis_size("harm")
    block_len = operating_point.shape[3]
    samples = coeffs * harm_count
    lower_face = field_in[:, faces[0]]
    upper_face = field_in[:, faces[1]]
    padded = with_halo(jnp.concatenate([lower_face, upper_face], axis=1), (("mesh", 1),), face_len)
    extended = jnp.concatenate([field_in, padded[:, :face_len], padded[:, 3 * face_len :]], axis=1)
    gathered = extended[:, connectivity]
    curl_part = jnp.einsum("ije,cje->cie", curl_vectors, gathered, precision=lax.Precision.HIGHEST)
    arrived = lax.all_to_all(
        lax.all_to_all(
            curl_part.reshape(coeffs, 3, mesh_count, 1, harm_count, 1, block_len),
            "mesh",
            split_axis=2,
            concat_axis=3,
            tiled=True,
        ),
        "harm",
        split_axis=4,
        concat_axis=5,
        tiled=True,
    )
    arrived = arrived.reshape(coeffs, 3, mesh_count, harm_count, block_len)
    inverse, forward = dft_tables(samples)
    inverse_blocks = inverse.reshape(samples, harm_count, coeffs)
    flux_step = jnp.einsum(
        "thk,kimhe->time", inverse_blocks, arrived, precision=lax.Precision.HIGHEST
    )
    field_step = apply_tensor(
        flux_step, operating_point, material, bh_knots, curve_base, curve_slopes
    )
    forward_blocks = forward.reshape(harm_count, coeffs, samples)
    outgoing = jnp.einsum(
        "hkt,time->kimhe", forward_blocks, field_step, precision=lax.Precision.HIGHEST
    )
    returned = lax.all_to_all(
        lax.all_to_all(
            outgoing.reshape(coeffs, 3, 1, mesh_count, 1, harm_count, block_len),
            "mesh",
            split_axis=3,
            concat_axis=2,
            tiled=True,
        ),
        "harm",
        split_axis=5,
        concat_axis=4,
        tiled=True,
    )
    field_part = returned.reshape(coeffs, 3, elements)
    contrib = jnp.einsum("ije,cie->cje", curl_vectors, field_part, precision=lax.Precision.HIGHEST)
    assembled = (
        jnp.zeros((coeffs, own_edges + 2 * face_len), jnp.float32)
        .at[:, connectivity.reshape(-1)]
        .add(contrib.reshape(coeffs, -1))
    )
    ghost_sums = with_halo(assembled[:, own_edges:], (("mesh", 1),), face_len)
    result = assembled[:, :own_edges].at[:, faces[0]].add(ghost_sums[:, :face_len])
    result = result.at[:, faces[1]].add(ghost_sums[:, 3 * face_len :])
    return result


def solution(mesh):
    return jax.shard_map(
        per_device,
        mesh=mesh,
        in_specs=(
            P("harm", "mesh"),
            P(None, "mesh"),
            P(None, "mesh"),
            P(None, None, "mesh"),
            P(None, None, None, ("mesh", "harm")),
            P(None, ("mesh", "harm")),
            P(),
            P(),
            P(),
        ),
        out_specs=P("harm", "mesh"),
        check_vma=False,
    )
```

profile of v0, /device:TPU:1, one launch (start us, length us, event | category | flops | bytes accessed | tf_op | source)
XLA Modules:
  0.0 467.0 jit_solution(17183202074254305449)
XLA Ops:
  2.6 4.0 gather_fusion
  9.2 4.0 gather_fusion.1
  14.8 6.7 %copy.84 = f32[3,6,4096]{1,0,2:T(4,128)} copy(f32[3,6,4096]{2,1,0:T(8,128)} %param.12) | data formatting | bytes 589824 | tf_op args[3]
  22.9 3.1 pad_maximum_fusion
  26.0 83.9 %gather_fusion.2 = f32[24576,16]{1,0:T(8,128)} fusion(f32[16,7168]{0,1:T(8,128)} %pad_maximum_fusion, s32[24576]{0:T(1024)S(1)} %broadcast_clamp_fusion), kind=kCustom, calls=%fused_computation.2 | custom fusion | bytes 3244032 | tf_op jit(solution)/shard_map/gather | solution.py:76
  109.9 39.5 %fusion = f32[4096,16,3]{1,2,0:T(4,128)} fusion(f32[3,6,4096]{1,0,2:T(4,128)} %copy.84, f32[6,4096,16]{2,1,0:T(8,128)} %bitcast.78), kind=kOutput, calls=%fused_computation.6 | convolution fusion | flops 14155776 | bytes 2654208 | tf_op jit(solution)/shard_map/ije,cje->cie/dot_general | solution.py:77
  149.3 7.5 %copy.85 = f32[16,3,8,1,4,1,128]{6,0,4,1,5,3,2:T(8,128)} copy(f32[16,3,8,1,4,1,128]{0,1,6,4,2,5,3:T(4,128)} %bitcast.77) | data formatting | bytes 1572864 | tf_op jit(solution)/shard_map/reshape | solution.py:80
  156.8 3.6 all-to-all-start
  160.9 8.6 %all-to-all-done = f32[16,3,8,1,4,1,128]{6,0,4,1,5,3,2:T(8,128)S(1)} async-done(((f32[16,3,8,1,4,1,128]{6,0,4,1,5,3,2:T(8,128)}), f32[16,3,8,1,4,1,128]{6,0,4,1,5,3,2:T(8,128)S(1)}, u32[]{:S(2)}, u32[]{:S(2)}) %all-to-all-start) | async-done | bytes 786464 | tf_op jit(solution)/shard_map/all_to_all | solution.py:79
  170.5 4.8 %all-to-all-start.1 = ((f32[16,3,1,8,4,1,128]{6,0,3,1,5,2,4:T(8,128)}), f32[16,3,1,8,4,1,128]{6,0,3,1,5,2,4:T(8,128)S(1)}, u32[]{:S(2)}, u32[]{:S(2)}) async-start(f32[16,3,1,8,4,1,128]{6,0,3,1,5,2,4:T(8,128)} %copy.86), calls=%async_computation.1 | async-start | bytes 1572864 | tf_op jit(solution)/shard_map/all_to_all | solution.py:78
  177.5 16.0 %all-to-all-done.1 = f32[16,3,1,8,4,1,128]{6,0,3,1,5,2,4:T(8,128)S(1)} async-done(((f32[16,3,1,8,4,1,128]{6,0,3,1,5,2,4:T(8,128)}), f32[16,3,1,8,4,1,128]{6,0,3,1,5,2,4:T(8,128)S(1)}, u32[]{:S(2)}, u32[]{:S(2)}) %all-to-all-start.1) | async-done | bytes 786464 | tf_op jit(solution)/shard_map/all_to_all | solution.py:78
  197.2 7.7 %all-to-all-start.2 = ((f32[16,3,1,8,1,4,128]{6,0,5,1,4,2,3:T(8,128)}), f32[16,3,1,8,1,4,128]{6,0,5,1,4,2,3:T(8,128)S(1)}, u32[]{:S(2)}, u32[]{:S(2)}) async-start(f32[16,3,1,8,1,4,128]{6,0,5,1,4,2,3:T(8,128)} %copy.92), calls=%async_computation.2 | async-start | bytes 1572864 | tf_op jit(solution)/shard_map/all_to_all | solution.py:105
  205.0 9.0 %all-to-all-done.2 = f32[16,3,1,8,1,4,128]{6,0,5,1,4,2,3:T(8,128)S(1)} async-done(((f32[16,3,1,8,1,4,128]{6,0,5,1,4,2,3:T(8,128)}), f32[16,3,1,8,1,4,128]{6,0,5,1,4,2,3:T(8,128)S(1)}, u32[]{:S(2)}, u32[]{:S(2)}) %all-to-all-start.2) | async-done | bytes 786464 | tf_op jit(solution)/shard_map/all_to_all | solution.py:105
  215.0 3.5 all-to-all-start.3
  218.6 18.7 %all-to-all-done.3 = f32[16,3,8,1,1,4,128]{6,0,2,1,4,3,5:T(8,128)S(1)} async-done(((f32[16,3,8,1,1,4,128]{6,0,2,1,4,3,5:T(8,128)}), f32[16,3,8,1,1,4,128]{6,0,2,1,4,3,5:T(8,128)S(1)}, u32[]{:S(2)}, u32[]{:S(2)}) %all-to-all-start.3) | async-done | bytes 786464 | tf_op jit(solution)/shard_map/all_to_all | solution.py:104
  237.3 5.8 %copy.105 = f32[16,3,8,1,1,4,128]{0,1,6,5,2,4,3:T(4,128)} copy(f32[16,3,8,1,1,4,128]{6,0,2,1,4,3,5:T(8,128)S(1)} %all-to-all-done.3) | data formatting | bytes 1572864 | tf_op jit(solution)/shard_map/reshape | solution.py:117
  243.1 37.0 %convolution_bitcast_fusion = f32[16,6,4096]{0,1,2:T(8,128)} fusion(f32[16,3,4096]{0,1,2:T(4,128)} %bitcast.79, f32[3,6,4096]{1,0,2:T(4,128)} %copy.84), kind=kOutput, calls=%fused_computation.9 | convolution fusion | flops 14155776 | bytes 2654208 | tf_op jit(solution)/shard_map/ije,cie->cje/dot_general | solution.py:118
  280.2 9.6 %copy.97 = f32[16,6,4096]{2,1,0:T(8,128)S(1)} copy(f32[16,6,4096]{0,1,2:T(8,128)} %convolution_bitcast_fusion) | data formatting | bytes 3145728 | tf_op jit(solution)/shard_map/ije,cie->cje/transpose | solution.py:118
  291.9 7.6 %copy.98 = f32[24576,16]{1,0:T(8,128)} copy(f32[24576,16]{0,1:T(8,128)} %bitcast.81) | data formatting | bytes 3145728 | tf_op jit(solution)/shard_map/reshape | solution.py:122
  299.5 132.9 %scatter_custom_fusion = f32[16,7168]{0,1:T(8,128)} fusion(s32[24576]{0:T(1024)S(1)} %bitcast.86, f32[24576,16]{1,0:T(8,128)} %copy.98, f32[]{:T(128)} %constant.23.clone.1), kind=kCustom, calls=%fused_computation.16 | custom fusion | flops 393216 | bytes 459264 | tf_op jit(solution)/shard_map/scatter-add | solution.py:122
  433.9 5.3 %collective-permute-start.2 = (f32[16,1024]{0,1:T(8,128)S(1)}, f32[16,1024]{0,1:T(8,128)}, u32[]{:S(2)}, u32[]{:S(2)}) collective-permute-start(f32[16,1024]{0,1:T(8,128)S(1)} %get-tuple-element.8), channel_id=1, source_target_pairs={{0,4},{4,8},{8,12},{12,16},{16,20},{20,24},{24,28},{28,0},{1,5},{5... | collective-permute-start | bytes 196616 | tf_op jit(solution)/shard_map/ppermute | solution.py:17
  439.2 11.5 %collective-permute-done.2 = f32[16,1024]{0,1:T(8,128)} collective-permute-done((f32[16,1024]{0,1:T(8,128)S(1)}, f32[16,1024]{0,1:T(8,128)}, u32[]{:S(2)}, u32[]{:S(2)}) %collective-permute-start.2) | collective-permute-done | bytes 65568 | tf_op jit(solution)/shard_map/ppermute | solution.py:17
  450.7 7.4 %scatter_custom_fusion.1 = f32[16,5120]{0,1:T(8,128)S(1)} fusion(f32[16,5120]{0,1:T(8,128)S(1)} %slice-done, s32[1024]{0:T(1024)S(1)} %bitcast.90, f32[16,1024]{0,1:T(8,128)} %collective-permute-done.2), kind=kCustom, calls=%fused_computation.33 | custom fusion | flops 16384 | bytes 393216 | tf_op jit(solution)/shard_map/scatter-add | solution.py:125
  458.1 7.4 %scatter_custom_fusion.2 = f32[16,5120]{0,1:T(8,128)S(1)} fusion(f32[16,5120]{0,1:T(8,128)S(1)} %scatter_custom_fusion.1, s32[1024]{0:T(1024)S(1)} %bitcast.88, f32[16,1024]{0,1:T(8,128)} %collective-permute-done.3), kind=kCustom, calls=%fused_computation.31 | custom fusion | flops 16384 | bytes 393216 | tf_op jit(solution)/shard_map/scatter-add | solution.py:126
  (52 shorter events, 21.4 us)
Async XLA Ops:
  0.0 160.5 %copy-start = (f32[4,8]{1,0:T(4,128)S(1)}, f32[4,8]{1,0:T(4,128)}, u32[]{:S(2)}) copy-start(f32[4,8]{1,0:T(4,128)} %param.17) | copy-start | bytes 388
  0.0 13.2 %copy-start.3 = (s32[6,4096]{1,0:T(8,128)S(1)}, s32[6,4096]{1,0:T(8,128)}, u32[]{:S(2)}) copy-start(s32[6,4096]{1,0:T(8,128)} %param.11) | copy-start | bytes 294916
  6.6 15.0 %collective-permute-start = (f32[16,1024]{0,1:T(8,128)}, f32[16,1024]{0,1:T(8,128)S(1)}, u32[]{:S(2)}, u32[]{:S(2)}) collective-permute-start(f32[16,1024]{0,1:T(8,128)} %bitcast.91), channel_id=1, source_target_pairs={{0,4},{4,8},{8,12},{12,16},{16,20},{20,24},{24,28},{28,0},{1,5},{5... | collective-permute-start | bytes 196616 | tf_op jit(solution)/shard_map/ppermute | solution.py:17
  13.2 9.7 %collective-permute-start.1 = (f32[16,1024]{0,1:T(8,128)}, f32[16,1024]{0,1:T(8,128)}, u32[]{:S(2)}, u32[]{:S(2)}) collective-permute-start(f32[16,1024]{0,1:T(8,128)} %bitcast.92), channel_id=1, source_target_pairs={{4,0},{8,4},{12,8},{16,12},{20,16},{24,20},{28,24},{0,28},{5,1},{9... | collective-permute-start | bytes 196616 | tf_op jit(solution)/shard_map/ppermute | solution.py:18
  149.3 11.2 %copy-start.4 = (s32[8,128]{1,0:T(8,128)S(1)}, s32[8,128]{1,0:T(8,128)}, u32[]{:S(2)}) copy-start(s32[8,128]{1,0:T(8,128)} %param.14) | copy-start | bytes 12292
  149.3 11.4 %copy-start.5 = (s32[8]{0:T(128)S(1)}, s32[8]{0:T(128)}, u32[]{:S(2)}) copy-start(s32[8]{0:T(128)} %param.15) | copy-start | bytes 100
  149.3 11.4 %copy-start.6 = (f32[4]{0:T(128)S(1)}, f32[4]{0:T(128)}, u32[]{:S(2)}) copy-start(f32[4]{0:T(128)} %param.16) | copy-start | bytes 52
  156.8 18.4 %copy-start.2 = (f32[64,3,8,128]{3,2,1,0:T(8,128)S(1)}, f32[64,3,8,128]{3,2,1,0:T(8,128)}, u32[]{:S(2)}) copy-start(f32[64,3,8,128]{3,2,1,0:T(8,128)} %param.13) | copy-start | bytes 2359300
  156.8 12.6 %all-to-all-start = ((f32[16,3,8,1,4,1,128]{6,0,4,1,5,3,2:T(8,128)}), f32[16,3,8,1,4,1,128]{6,0,4,1,5,3,2:T(8,128)S(1)}, u32[]{:S(2)}, u32[]{:S(2)}) async-start(f32[16,3,8,1,4,1,128]{6,0,4,1,5,3,2:T(8,128)} %copy.85), calls=%async_computation | async-start | bytes 1572864 | tf_op jit(solution)/shard_map/all_to_all | solution.py:79
  170.5 23.0 %all-to-all-start.1 = ((f32[16,3,1,8,4,1,128]{6,0,3,1,5,2,4:T(8,128)}), f32[16,3,1,8,4,1,128]{6,0,3,1,5,2,4:T(8,128)S(1)}, u32[]{:S(2)}, u32[]{:S(2)}) async-start(f32[16,3,1,8,4,1,128]{6,0,3,1,5,2,4:T(8,128)} %copy.86), calls=%async_computation.1 | async-start | bytes 1572864 | tf_op jit(solution)/shard_map/all_to_all | solution.py:78
  197.2 16.9 %all-to-all-start.2 = ((f32[16,3,1,8,1,4,128]{6,0,5,1,4,2,3:T(8,128)}), f32[16,3,1,8,1,4,128]{6,0,5,1,4,2,3:T(8,128)S(1)}, u32[]{:S(2)}, u32[]{:S(2)}) async-start(f32[16,3,1,8,1,4,128]{6,0,5,1,4,2,3:T(8,128)} %copy.92), calls=%async_computation.2 | async-start | bytes 1572864 | tf_op jit(solution)/shard_map/all_to_all | solution.py:105
  215.0 22.3 %all-to-all-start.3 = ((f32[16,3,8,1,1,4,128]{6,0,2,1,4,3,5:T(8,128)}), f32[16,3,8,1,1,4,128]{6,0,2,1,4,3,5:T(8,128)S(1)}, u32[]{:S(2)}, u32[]{:S(2)}) async-start(f32[16,3,8,1,1,4,128]{6,0,2,1,4,3,5:T(8,128)} %copy.93), calls=%async_computation.3 | async-start | bytes 1572864 | tf_op jit(solution)/shard_map/all_to_all | solution.py:104
  432.4 18.2 %slice-start = ((f32[16,7168]{0,1:T(8,128)}), f32[16,5120]{0,1:T(8,128)S(1)}, s32[]{:S(2)}) async-start(f32[16,7168]{0,1:T(8,128)} %scatter_custom_fusion), calls=%async_computation.4 | async-start | bytes 5242880 | tf_op jit(solution)/shard_map/slice | solution.py:125
  433.9 16.8 %collective-permute-start.2 = (f32[16,1024]{0,1:T(8,128)S(1)}, f32[16,1024]{0,1:T(8,128)}, u32[]{:S(2)}, u32[]{:S(2)}) collective-permute-start(f32[16,1024]{0,1:T(8,128)S(1)} %get-tuple-element.8), channel_id=1, source_target_pairs={{0,4},{4,8},{8,12},{12,16},{16,20},{20,24},{24,28},{28,0},{1,5},{5... | collective-permute-start | bytes 196616 | tf_op jit(solution)/shard_map/ppermute | solution.py:17
  439.2 18.9 %collective-permute-start.3 = (f32[16,1024]{0,1:T(8,128)S(1)}, f32[16,1024]{0,1:T(8,128)}, u32[]{:S(2)}, u32[]{:S(2)}) collective-permute-start(f32[16,1024]{0,1:T(8,128)S(1)} %get-tuple-element.7), channel_id=1, source_target_pairs={{4,0},{8,4},{12,8},{16,12},{20,16},{24,20},{28,24},{0,28},{5,1},{9... | collective-permute-start | bytes 196616 | tf_op jit(solution)/shard_map/ppermute | solution.py:18
  450.7 16.3 %copy-start.1 = (f32[4,8]{1,0:T(4,128)S(1)}, f32[4,8]{1,0:T(4,128)}, u32[]{:S(2)}) copy-start(f32[4,8]{1,0:T(4,128)} %param.17) | copy-start | bytes 388
where the time goes:
time: 468 us; the launch traced here: 467 us
  other arithmetic  155 us (33%)
  local copies, waits for them, and re-layouts  140 us (30%)
  matrix products  79.3 us (17%)
  waiting for transfers between devices  65.2 us (14%)
  starting transfers between devices  27.6 us (6%)
    scatter-add x1, other arithmetic, per_device(): assembled = jnp.zeros((coeffs, own_edges + 2 * face_len), jnp.float32).at...  133 us
    gather x1, local copies, waits for them, and re-layouts, per_device(): gathered = extended[:, connectivity]  83.9 us
    dot_general x1, matrix products, per_device(): jnp.einsum('ije,cje->cie', curl_vectors, gathered, precision=lax.Precisio...  39.5 us
    dot_general x1, matrix products, per_device(): jnp.einsum('ije,cie->cje', curl_vectors, field_part, precision=lax.Precis...  37 us
    all_to_all x1, waiting for transfers between devices, per_device(): lax.all_to_all(lax.all_to_all(outgoing.reshape(coeffs, 3, 1, mesh_count,...  18.7 us
    all_to_all x1, waiting for transfers between devices, per_device(): lax.all_to_all(lax.all_to_all(curl_part.reshape(coeffs, 3, mesh_count, 1,...  16 us
    ppermute x2, waiting for transfers between devices, with_halo(): before = lax.ppermute(last, axis, up)  11.5 us
    unnamed x18, local copies, waits for them, and re-layouts  10.7 us
  transfers between devices with their start and end apart: 8, of which 6 were waited for; matrix products, arithmetic and copies ran while one was open for 5% of the time, Pallas kernels for 0%

commit v1 on v0

v1 whole, which is shorter than its diff:
```python
import functools

import jax
import jax.numpy as jnp
import numpy as np
from jax import lax
from jax.experimental import pallas as pl
from jax.experimental.pallas import tpu as pltpu
from jax.sharding import PartitionSpec as P

KNOT_STEP = 0.25
KNOT_WIDTH = 0.5
WIDE = 256
SHIFT = 8
BF = jnp.bfloat16
F32 = jnp.float32
VM = pl.BlockSpec(memory_space=pltpu.VMEM)
SM = pl.BlockSpec(memory_space=pltpu.SMEM)
NT = (((1,), (1,)), ((), ()))


def dft_tables(length):
    coef = np.arange(length)
    half = length // 2
    harmonic = np.where(coef < half, coef, coef - half + 1)
    harmonic = np.where(coef == length - 1, half, harmonic)
    is_sine = (coef >= half) & (coef < length - 1)
    angles = (harmonic[:, None] * coef[None, :] % length) * (2.0 * np.pi / length)
    rows = np.where(is_sine[:, None], np.sin(angles), np.cos(angles))
    weight = np.where((coef == 0) | (coef == length - 1), 1.0 / length, 2.0 / length)
    return rows.T.astype(np.float32), (rows * weight[:, None]).astype(np.float32)


def split(value):
    high = value.astype(BF)
    return high, (value - high.astype(F32)).astype(BF)


def cost(flops):
    return pl.CostEstimate(flops=flops, bytes_accessed=4 << 20, transcendentals=0)


def fill_tiles(source_ref, tiles):
    rows, columns = source_ref.shape
    for tile in range(columns // WIDE):
        high, low = split(source_ref[:, tile * WIDE : (tile + 1) * WIDE])
        tiles[tile * rows : (tile + 1) * rows, :WIDE] = high
        tiles[tile * rows : (tile + 1) * rows, WIDE:] = low


def one_hot(ids, iota):
    low = jnp.bitwise_and(ids, WIDE - 1)
    return (jnp.broadcast_to(low, iota.shape) == iota).astype(F32).astype(BF)


def pick(tiles, ids, iota, rows, first):
    hot = one_hot(ids, iota)
    table = jnp.dot(tiles[:, :WIDE], hot, preferred_element_type=F32)
    table = table + jnp.dot(tiles[:, WIDE:], hot, preferred_element_type=F32)
    tile_of = jnp.broadcast_to(jnp.right_shift(ids, SHIFT), (rows, ids.shape[1]))
    found = jnp.zeros((rows, ids.shape[1]), F32)
    for tile in range(tiles.shape[0] // rows):
        found = jnp.where(tile_of == tile + first, table[tile * rows : (tile + 1) * rows], found)
    return found


def spread(value, ids, iota, first, count):
    rows = value.shape[0]
    high, low = split(value)
    hot = one_hot(ids, iota)
    tile_of = jnp.broadcast_to(jnp.right_shift(ids, SHIFT), value.shape).astype(F32).astype(BF)
    zero = jnp.zeros_like(high)
    total = None
    for part in (high, low):
        left = jnp.concatenate(
            [jnp.where(tile_of == BF(tile + first), part, zero) for tile in range(count)], axis=0
        )
        term = lax.dot_general(left, hot, NT, preferred_element_type=F32)
        total = term if total is None else total + term
    return total


def face_kernel(source_ref, faces_ref, lower_ref, upper_ref, tiles, *, width):
    rows = source_ref.shape[0]
    fill_tiles(source_ref, tiles)
    iota = lax.broadcasted_iota(jnp.int32, (WIDE, width), 0)
    for side, out_ref in enumerate((lower_ref, upper_ref)):
        for start in range(0, faces_ref.shape[1], width):
            ids = faces_ref[side : side + 1, start : start + width]
            out_ref[:, start : start + width] = pick(tiles, ids, iota, rows, 0)


def curl_kernel(*refs, width, first, sources, added):
    source_refs = refs[:sources]
    ids_ref, curl_ref = refs[sources : sources + 2]
    prior_ref = refs[sources + 2] if added else None
    out_ref, tiles = refs[-2:]
    rows = source_refs[0].shape[0]
    start = 0
    for source_ref in source_refs:
        size = source_ref.shape[1] // WIDE * rows
        fill_tiles(source_ref, tiles.at[start : start + size])
        start += size
    blocks, nodes, length = ids_ref.shape
    steps = length // width
    iota = lax.broadcasted_iota(jnp.int32, (WIDE, width), 0)

    def body(step, carry):
        block = step // steps
        column = pl.multiple_of(step % steps * width, width)
        window = pl.ds(column, width)
        sums = [prior_ref[block, i, :, window] if added else None for i in range(3)]
        for j in range(nodes):
            found = pick(tiles, ids_ref[block, pl.ds(j, 1), window], iota, rows, first)
            for i in range(3):
                weight = jnp.broadcast_to(curl_ref[block, i, pl.ds(j, 1), window], found.shape)
                sums[i] = weight * found if sums[i] is None else sums[i] + weight * found
        for i in range(3):
            out_ref[block, i, :, window] = sums[i]
        return carry

    lax.fori_loop(0, blocks * steps, body, 0)


def curls(sources, ids, curl, first, prior=None):
    rows = sources[0].shape[0]
    blocks, nodes, length = ids.shape
    width = min(512, length)
    tiles = sum(s.shape[1] for s in sources) // WIDE
    extra = () if prior is None else (prior,)
    return pl.pallas_call(
        functools.partial(
            curl_kernel, width=width, first=first, sources=len(sources), added=prior is not None
        ),
        out_shape=jax.ShapeDtypeStruct((blocks, 3, rows, length), F32),
        in_specs=[VM] * (len(sources) + 2 + len(extra)),
        out_specs=VM,
        scratch_shapes=[pltpu.VMEM((tiles * rows, 2 * WIDE), BF)],
        cost_estimate=cost(tiles * rows * WIDE * 4 * blocks * nodes * length),
    )(*sources, ids, curl, *extra)


def assemble_kernel(field_ref, ids_ref, curl_ref, *refs, width, first, counts):
    out_refs, sums = refs[:-1], refs[-1]
    blocks, _, rows, length = field_ref.shape
    nodes = ids_ref.shape[1]
    steps = length // width
    count = sum(counts)
    sums[...] = jnp.zeros_like(sums)
    iota = lax.broadcasted_iota(jnp.int32, (WIDE, width), 0)

    def body(step, carry):
        block = step // steps
        column = pl.multiple_of(step % steps * width, width)
        window = pl.ds(column, width)
        field = [field_ref[block, i, :, window] for i in range(3)]
        total = None
        for j in range(nodes):
            value = None
            for i in range(3):
                weight = jnp.broadcast_to(curl_ref[block, i, pl.ds(j, 1), window], field[i].shape)
                value = weight * field[i] if value is None else value + weight * field[i]
            term = spread(value, ids_ref[block, pl.ds(j, 1), window], iota, first, count)
            total = term if total is None else total + term
        sums[...] += total
        return carry

    lax.fori_loop(0, blocks * steps, body, 0)
    tile = 0
    for out_ref, number in zip(out_refs, counts):
        for part in range(number):
            out_ref[:, part * WIDE : (part + 1) * WIDE] = sums[tile * rows : (tile + 1) * rows, :]
            tile += 1


def assemble(field, ids, curl, first, counts):
    blocks, _, rows, length = field.shape
    width = min(512, length)
    tiles = sum(counts)
    return pl.pallas_call(
        functools.partial(assemble_kernel, width=width, first=first, counts=counts),
        out_shape=[jax.ShapeDtypeStruct((rows, n * WIDE), F32) for n in counts],
        in_specs=[VM] * 3,
        out_specs=[VM] * len(counts),
        scratch_shapes=[pltpu.VMEM((tiles * rows, WIDE), F32)],
        cost_estimate=cost(tiles * rows * WIDE * 4 * blocks * ids.shape[1] * length),
    )(field, ids, curl)


def finish_kernel(own_ref, below_ref, above_ref, faces_ref, out_ref, *, width):
    rows, columns = own_ref.shape
    count = columns // WIDE
    iota = lax.broadcasted_iota(jnp.int32, (WIDE, width), 0)
    total = None
    for side, value_ref in enumerate((below_ref, above_ref)):
        for start in range(0, faces_ref.shape[1], width):
            window = slice(start, start + width)
            term = spread(value_ref[:, window], faces_ref[side : side + 1, window], iota, 0, count)
            total = term if total is None else total + term
    for tile in range(count):
        window = slice(tile * WIDE, (tile + 1) * WIDE)
        out_ref[:, window] = own_ref[:, window] + total[tile * rows : (tile + 1) * rows]


def curve_kernel(knots_ref, base_ref, slopes_ref, point_ref, nu_ref, twice_ref):
    samples, length = nu_ref.shape
    kinds = base_ref.shape[0]
    material = point_ref[3 * samples : 3 * samples + 1, :]
    masks = [material == float(kind) for kind in range(1, kinds)]

    def select(values):
        chosen = jnp.full((1, length), values[0], F32)
        for mask, value in zip(masks, values[1:]):
            chosen = jnp.where(mask, value, chosen)
        return chosen

    base = select([base_ref[kind] for kind in range(kinds)])
    knots = knots_ref.shape[0]
    slopes = [select([slopes_ref[kind, k] for kind in range(kinds)]) for k in range(knots)]
    starts = [knots_ref[k].astype(F32) * KNOT_STEP for k in range(knots)]

    def body(step, carry):
        row = pl.multiple_of(step * 8, 8)
        b = [point_ref[pl.ds(i * samples + row, 8), :] for i in range(3)]
        square = b[0] * b[0] + b[1] * b[1] + b[2] * b[2]
        nu = jnp.broadcast_to(base, square.shape)
        slope = jnp.zeros_like(square)
        for k in range(knots):
            z = (square - starts[k]) * (1.0 / KNOT_WIDTH)
            decay = jnp.exp(-jnp.abs(z))
            weight = jnp.broadcast_to(slopes[k], z.shape)
            nu = nu + weight * (jnp.maximum(z, 0.0) + jnp.log1p(decay))
            slope = slope + weight * (jnp.where(z >= 0.0, 1.0, decay) / (1.0 + decay))
        nu_ref[pl.ds(row, 8), :] = nu
        twice_ref[pl.ds(row, 8), :] = slope * (2.0 / KNOT_WIDTH)
        return carry

    lax.fori_loop(0, samples // 8, body, 0)


def tensor_kernel(flux_ref, point_ref, nu_ref, twice_ref, inverse_ref, forward_ref, out_ref):
    blocks, _, rows, length = flux_ref.shape
    samples = blocks * rows
    dot = functools.partial(
        jnp.dot, precision=lax.Precision.HIGHEST, preferred_element_type=F32
    )
    width = min(256, length)
    for start in range(0, length, width):
        window = slice(start, start + width)
        b = [point_ref[i * samples : (i + 1) * samples, window] for i in range(3)]
        flux = []
        for i in range(3):
            packed = jnp.concatenate([flux_ref[k, i, :, window] for k in range(blocks)], axis=0)
            flux.append(dot(inverse_ref[...], packed))
        along = b[0] * flux[0] + b[1] * flux[1] + b[2] * flux[2]
        along = along * twice_ref[:, window]
        nu = nu_ref[:, window]
        for i in range(3):
            coefs = dot(forward_ref[...], nu * flux[i] + along * b[i])
            for k in range(blocks):
                out_ref[k, i, :, window] = coefs[k * rows : (k + 1) * rows]


def per_device(
    field_in,
    faces,
    connectivity,
    curl_vectors,
    operating_point,
    material,
    bh_knots,
    curve_base,
    curve_slopes,
):
    rows, own = field_in.shape
    face_len = faces.shape[1]
    nodes, elements = connectivity.shape
    mesh_count = lax.axis_size("mesh")
    harm_count = lax.axis_size("harm")
    block = operating_point.shape[3]
    samples = operating_point.shape[0]
    length = elements // harm_count
    up = [(i, (i + 1) % mesh_count) for i in range(mesh_count)]
    down = [(j, i) for i, j in up]

    points = jnp.transpose(operating_point, (2, 1, 0, 3)).reshape(mesh_count, 3 * samples, block)
    kinds = jnp.broadcast_to(material.astype(F32)[:, None, :], (mesh_count, 8, block))
    points = jnp.concatenate([points, kinds], axis=1)
    points = lax.all_to_all(points, "mesh", split_axis=0, concat_axis=0, tiled=True)
    points = jnp.transpose(points, (1, 0, 2)).reshape(3 * samples + 8, length)

    ids = connectivity.reshape(nodes, mesh_count, harm_count, block)
    ids = jnp.transpose(ids, (2, 0, 1, 3)).reshape(harm_count, nodes, length)
    curl = curl_vectors.reshape(3, nodes, mesh_count, harm_count, block)
    curl = jnp.transpose(curl, (3, 0, 1, 2, 4)).reshape(harm_count, 3, nodes, length)

    face_width = min(512, face_len)
    own_tiles, face_tiles = own // WIDE, face_len // WIDE
    face_shape = jax.ShapeDtypeStruct((rows, face_len), F32)
    lower, upper = pl.pallas_call(
        functools.partial(face_kernel, width=face_width),
        out_shape=[face_shape, face_shape],
        in_specs=[VM] * 2,
        out_specs=[VM] * 2,
        scratch_shapes=[pltpu.VMEM((own_tiles * rows, 2 * WIDE), BF)],
        cost_estimate=cost(own * rows * 8 * face_len),
    )(field_in, faces)
    before = lax.ppermute(upper, "mesh", up)
    after = lax.ppermute(lower, "mesh", down)

    partial = curls([field_in], ids, curl, 0)
    flux = curls([before, after], ids, curl, own_tiles, partial)
    flux = lax.all_to_all(flux, "harm", split_axis=0, concat_axis=0, tiled=True)

    plane = jax.ShapeDtypeStruct((samples, length), F32)
    nu, twice = pl.pallas_call(
        curve_kernel,
        out_shape=[plane, plane],
        in_specs=[SM] * 3 + [VM],
        out_specs=[VM] * 2,
        cost_estimate=cost(samples * length * 8 * 40),
    )(bh_knots, curve_base, curve_slopes, points)

    inverse, forward = dft_tables(samples)
    field = pl.pallas_call(
        tensor_kernel,
        out_shape=jax.ShapeDtypeStruct(flux.shape, F32),
        in_specs=[VM] * 6,
        out_specs=VM,
        cost_estimate=cost(samples * samples * length * 6 * 12),
    )(flux, points, nu, twice, inverse, forward)
    field = lax.all_to_all(field, "harm", split_axis=0, concat_axis=0, tiled=True)

    low_sums, high_sums = assemble(field, ids, curl, own_tiles, (face_tiles, face_tiles))
    above = lax.ppermute(low_sums, "mesh", down)
    below = lax.ppermute(high_sums, "mesh", up)
    (own_sums,) = assemble(field, ids, curl, 0, (own_tiles,))
    return pl.pallas_call(
        functools.partial(finish_kernel, width=face_width),
        out_shape=jax.ShapeDtypeStruct((rows, own), F32),
        in_specs=[VM] * 4,
        out_specs=VM,
        cost_estimate=cost(own * rows * 8 * face_len),
    )(own_sums, below, above, faces)


def solution(mesh):
    return jax.shard_map(
        per_device,
        mesh=mesh,
        in_specs=(
            P("harm", "mesh"),
            P(None, "mesh"),
            P(None, "mesh"),
            P(None, None, "mesh"),
            P(None, None, None, ("mesh", "harm")),
            P(None, ("mesh", "harm")),
            P(),
            P(),
            P(),
        ),
        out_specs=P("harm", "mesh"),
        check_vma=False,
    )
```

time: 468 us -> 124 us (0.26)
  other arithmetic: 155 us -> 0.94 us
  local copies, waits for them, and re-layouts: 140 us -> 6.73 us
  matrix products: 79.3 us -> 0 us
  Pallas kernels: 0 us -> 60.4 us
  waiting for transfers between devices: 65.2 us -> 14.9 us
  blocking collectives: 0 us -> 23.4 us
  starting transfers between devices: 27.6 us -> 15.4 us
    scatter-add x3 -> x0, other arithmetic: 148 us -> none  [the longest x1 133 us: per_device(): assembled = jnp.zeros((coeffs, own_edges + 2 * face_len), jnp.float32).at...]
    gather x3 -> x0, local copies, waits for them, and re-layouts: 92 us -> none  [the longest x1 83.9 us: per_device(): gathered = extended[:, connectivity]]
    dot_general x6 -> x0, matrix products: 79.3 us -> none  [the longest x1 39.5 us: per_device(): jnp.einsum('ije,cje->cie', curl_vectors, gathered, precision=lax.Precisio...]
    pallas_call x0 -> x8, Pallas kernels: none -> 60.4 us  [the longest x2 23.9 us: assemble(): pl.pallas_call(functools.partial(assemble_kernel, width=width, first=firs...]
    all_to_all x4 -> x2, waiting for transfers between devices: 52.4 us -> 14.9 us  [the longest x1 14.9 us: per_device(): flux = lax.all_to_all(flux, 'harm', split_axis=0, concat_axis=0, tiled=True)]
    all_to_all x0 -> x1, blocking collectives: none -> 23.4 us  [per_device(): lax.all_to_all(field, 'harm', split_axis=0, concat_axis=0, tiled=True)]
    reshape x4 -> x9, local copies, waits for them, and re-layouts: 21.9 us -> 3.07 us  [the longest x2 1.04 us: per_device(): jnp.transpose(curl, (3, 0, 1, 2, 4)).reshape(harm_count, 3, nodes, length)]
    ppermute x4, waiting for transfers between devices: 12.8 us -> 0.01 us  [the longest x1 0.01 us: per_device(): before = lax.ppermute(upper, 'mesh', up)]
  transfers between devices with their start and end apart: 8 -> 6, of which waited for: 6 -> 1; matrix products, arithmetic and copies ran while one was open for 5% -> 3% of each run, Pallas kernels for 0% -> 32%
where the time goes in v1:
time: 124 us; the launch traced here: 122 us
  Pallas kernels  60.4 us (49%)
  blocking collectives  23.4 us (19%)
  starting transfers between devices  15.4 us (12%)
  waiting for transfers between devices  14.9 us (12%)
  local copies, waits for them, and re-layouts  6.73 us (5%)
    pallas_call x2, Pallas kernels, assemble(): pl.pallas_call(functools.partial(assemble_kernel, width=width, first=firs...  23.9 us
    all_to_all x1, blocking collectives, per_device(): lax.all_to_all(field, 'harm', split_axis=0, concat_axis=0, tiled=True)  23.4 us
    pallas_call x2, Pallas kernels, curls(): pl.pallas_call(functools.partial(curl_kernel, width=width, first=first, s...  22.7 us
    all_to_all x1, waiting for transfers between devices, per_device(): flux = lax.all_to_all(flux, 'harm', split_axis=0, concat_axis=0, tiled=True)  14.9 us
    all_to_all x1, starting transfers between devices, per_device(): flux = lax.all_to_all(flux, 'harm', split_axis=0, concat_axis=0, tiled=True)  5.21 us
    pallas_call x1, Pallas kernels, per_device(): pl.pallas_call(tensor_kernel, out_shape=jax.ShapeDtypeStruct(flux.shape,...  4.57 us
    all_to_all x1, starting transfers between devices, per_device(): lax.all_to_all(points, 'mesh', split_axis=0, concat_axis=0, tiled=True)  4.48 us
    pallas_call x1, Pallas kernels, per_device(): pl.pallas_call(curve_kernel, out_shape=[plane, plane], in_specs=[SM] * 3...  3.95 us
  transfers between devices with their start and end apart: 6, of which 1 were waited for; matrix products, arithmetic and copies ran while one was open for 3% of the time, Pallas kernels for 32%

profile of v1, /device:TPU:1, one launch (start us, length us, event | category | flops | bytes accessed | tf_op | source)
XLA Modules:
  0.0 121.8 jit_solution(49274528642671622)
XLA Ops:
  0.0 2.7 %shard_map.109 = (f32[16,1024]{1,0:T(8,128)}, f32[16,1024]{1,0:T(8,128)}) custom-call(f32[16,5120]{1,0:T(8,128)} %refs_0_.1, s32[2,1024]{1,0:T(2,128)} %faces_ref.3), custom_call_target="tpu_custom_call" | custom-call | flops 671088640 | bytes 4194304 | tf_op jit(solution)/shard_map/pallas_call | solution.py:300
  2.7 2.6 %collective-permute-start = (f32[16,1024]{1,0:T(8,128)}, f32[16,1024]{1,0:T(8,128)S(1)}, u32[]{:S(2)}, u32[]{:S(2)}) collective-permute-start(f32[16,1024]{1,0:T(8,128)} %get-tuple-element.11), channel_id=1, source_target_pairs={{0,4},{4,8},{8,12},{12,16},{16,20},{20,24},{24,28},{28,0},{1,5},{5... | collective-permute-start | bytes 196616 | tf_op jit(solution)/shard_map/ppermute | solution.py:308
  5.4 0.9 pad_maximum_fusion
  6.4 4.5 %all-to-all-start.1 = ((f32[8,200,128]{2,1,0:T(8,128)}), f32[8,200,128]{2,1,0:T(8,128)S(1)}, u32[]{:S(2)}, u32[]{:S(2)}) async-start(f32[8,200,128]{2,1,0:T(8,128)} %pad_maximum_fusion), calls=%async_computation.1 | async-start | bytes 1638400 | tf_op jit(solution)/shard_map/all_to_all | solution.py:289
  11.0 0.7 copy.18.refs_1_.refs_2_.ids_ref
  11.9 0.2 reshape.21
  12.2 0.9 copy.19.refs_2_.refs_3_.curl_ref
  13.1 13.7 %shard_map.110.refs_4_ = f32[4,3,16,1024]{3,2,1,0:T(8,128)} custom-call(f32[16,5120]{1,0:T(8,128)} %refs_0_.1, s32[4,6,1024]{2,1,0:T(8,128)} %copy.18.refs_1_.refs_2_.ids_ref, f32[4,3,6,1024]{3,2,1,0:T(8,128)} %copy.19.refs_2_.refs_3_.curl_ref), custom_call_target="tpu_custom_call" | custom-call | flops 8053063680 | bytes 4194304 | tf_op jit(solution)/shard_map/pallas_call | solution.py:131
  26.8 0.6 copy-done.5
  27.4 0.6 copy-done.6
  28.1 9.0 %shard_map.111 = f32[4,3,16,1024]{3,2,1,0:T(8,128)} custom-call(f32[16,1024]{1,0:T(8,128)} %copy-done.5, f32[16,1024]{1,0:T(8,128)} %copy-done.6, s32[4,6,1024]{2,1,0:T(8,128)} %copy.18.refs_1_.refs_2_.ids_ref, f32[4,3,6,1024]{3,2,1,0:T(8,128)} %copy.19.refs_2_.refs_3_.curl_ref, f32[4,3,16,1024]{3,2,1,0:T(8,128)} %shard_map.110.refs_4_), custom_call_target="tpu_custom_call" | custom-call | flops 3221225472 | bytes 4194304 | tf_op jit(solution)/shard_map/pallas_call | solution.py:131
  37.1 5.2 %all-to-all-start = ((f32[4,3,16,1024]{3,2,1,0:T(8,128)}), f32[4,3,16,1024]{3,2,1,0:T(8,128)S(1)}, u32[]{:S(2)}, u32[]{:S(2)}) async-start(f32[4,3,16,1024]{3,2,1,0:T(8,128)} %shard_map.111), calls=%async_computation | async-start | bytes 1572864 | tf_op jit(solution)/shard_map/all_to_all | solution.py:313
  42.3 1.0 copy_bitcast_fusion.point_ref
  43.3 3.9 %shard_map.112 = (f32[64,1024]{1,0:T(8,128)}, f32[64,1024]{1,0:T(8,128)}) custom-call(s32[8]{0:T(128)} %knots_ref.1, f32[4]{0:T(128)} %base_ref.1, f32[4,8]{1,0:T(4,128)} %slopes_ref.1, f32[200,1024]{1,0:T(8,128)} %copy_bitcast_fusion.point_ref), custom_call_target="tpu_custom_call" | custom-call | flops 20971520 | bytes 4194304 | tf_op jit(solution)/shard_map/pallas_call | solution.py:316
  47.2 14.9 %all-to-all-done.flux_ref = f32[4,3,16,1024]{3,2,1,0:T(8,128)S(1)} async-done(((f32[4,3,16,1024]{3,2,1,0:T(8,128)}), f32[4,3,16,1024]{3,2,1,0:T(8,128)S(1)}, u32[]{:S(2)}, u32[]{:S(2)}) %all-to-all-start) | async-done | bytes 786464 | tf_op jit(solution)/shard_map/all_to_all | solution.py:313
  62.1 0.9 copy-done
  63.0 4.6 %shard_map.113 = f32[4,3,16,1024]{3,2,1,0:T(8,128)} custom-call(f32[4,3,16,1024]{3,2,1,0:T(8,128)} %copy-done, f32[200,1024]{1,0:T(8,128)} %copy_bitcast_fusion.point_ref, f32[64,1024]{1,0:T(8,128)} %get-tuple-element.13.nu_ref, f32[64,1024]{1,0:T(8,128)} %get-tuple-element.14.twice_ref, f32[64,64]{1,0:T(8,128)} %constant.4.clone.inverse_ref, ...), custom_call_target="tpu_custom_call" | custom-call | flops 301989888 | bytes 4194304 | tf_op jit(solution)/shard_map/pallas_call | solution.py:325
  67.5 23.4 %all_to_all.15.field_ref = f32[4,3,16,1024]{3,2,1,0:T(8,128)} all-to-all(f32[4,3,16,1024]{3,2,1,0:T(8,128)} %shard_map.113), channel_id=1, replica_groups=mesh['mesh'=8,'harm'=4] {'harm'}, dimensions={0} | all-to-all | bytes 1572864 | tf_op jit(solution)/shard_map/all_to_all | solution.py:332
  90.9 11.7 %shard_map.115 = (f32[16,1024]{1,0:T(8,128)}, f32[16,1024]{1,0:T(8,128)}) custom-call(f32[4,3,16,1024]{3,2,1,0:T(8,128)} %all_to_all.15.field_ref, s32[4,6,1024]{2,1,0:T(8,128)} %copy.18.refs_1_.refs_2_.ids_ref, f32[4,3,6,1024]{3,2,1,0:T(8,128)} %copy.19.refs_2_.refs_3_.curl_ref), custom_call_target="tpu_custom_call" | custom-call | flops 3221225472 | bytes 4194304 | tf_op jit(solution)/shard_map/pallas_call | solution.py:180
  102.6 3.1 %collective-permute-start.2 = (f32[16,1024]{1,0:T(8,128)}, f32[16,1024]{1,0:T(8,128)S(1)}, u32[]{:S(2)}, u32[]{:S(2)}) collective-permute-start(f32[16,1024]{1,0:T(8,128)} %get-tuple-element.15), channel_id=1, source_target_pairs={{0,4},{4,8},{8,12},{12,16},{16,20},{20,24},{24,28},{28,0},{1,5},{5... | collective-permute-start | bytes 196616 | tf_op jit(solution)/shard_map/ppermute | solution.py:336
  105.7 12.2 %shard_map.114.own_ref = f32[16,5120]{1,0:T(8,128)} custom-call(f32[4,3,16,1024]{3,2,1,0:T(8,128)} %all_to_all.15.field_ref, s32[4,6,1024]{2,1,0:T(8,128)} %copy.18.refs_1_.refs_2_.ids_ref, f32[4,3,6,1024]{3,2,1,0:T(8,128)} %copy.19.refs_2_.refs_3_.curl_ref), custom_call_target="tpu_custom_call" | custom-call | flops 8053063680 | bytes 4194304 | tf_op jit(solution)/shard_map/pallas_call | solution.py:180
  117.9 0.6 copy-done.7
  118.5 0.6 copy-done.8
  119.1 2.6 %shard_map.116 = f32[16,5120]{1,0:T(8,128)} custom-call(f32[16,5120]{1,0:T(8,128)} %shard_map.114.own_ref, f32[16,1024]{1,0:T(8,128)} %copy-done.7, f32[16,1024]{1,0:T(8,128)} %copy-done.8, s32[2,1024]{1,0:T(2,128)} %faces_ref.3), custom_call_target="tpu_custom_call" | custom-call | flops 671088640 | bytes 4194304 | tf_op jit(solution)/shard_map/pallas_call | solution.py:338
  (28 shorter events, 0.6 us)
Async XLA Ops:
  0.0 5.3 %copy-start.1 = (f32[64,3,8,128]{3,2,1,0:T(8,128)S(1)}, f32[64,3,8,128]{3,2,1,0:T(8,128)}, u32[]{:S(2)}) copy-start(f32[64,3,8,128]{3,2,1,0:T(8,128)} %param.15) | copy-start | bytes 2359300
  0.0 5.3 %copy-start.4 = (s32[8,128]{1,0:T(8,128)S(1)}, s32[8,128]{1,0:T(8,128)}, u32[]{:S(2)}) copy-start(s32[8,128]{1,0:T(8,128)} %param.16) | copy-start | bytes 12292
  2.7 24.2 %collective-permute-start = (f32[16,1024]{1,0:T(8,128)}, f32[16,1024]{1,0:T(8,128)S(1)}, u32[]{:S(2)}, u32[]{:S(2)}) collective-permute-start(f32[16,1024]{1,0:T(8,128)} %get-tuple-element.11), channel_id=1, source_target_pairs={{0,4},{4,8},{8,12},{12,16},{16,20},{20,24},{24,28},{28,0},{1,5},{5... | collective-permute-start | bytes 196616 | tf_op jit(solution)/shard_map/ppermute | solution.py:308
  5.3 21.6 %collective-permute-start.1 = (f32[16,1024]{1,0:T(8,128)}, f32[16,1024]{1,0:T(8,128)S(1)}, u32[]{:S(2)}, u32[]{:S(2)}) collective-permute-start(f32[16,1024]{1,0:T(8,128)} %get-tuple-element.12), channel_id=1, source_target_pairs={{4,0},{8,4},{12,8},{16,12},{20,16},{24,20},{28,24},{0,28},{5,1},{9... | collective-permute-start | bytes 196616 | tf_op jit(solution)/shard_map/ppermute | solution.py:309
  6.4 4.5 %copy-start.3 = (s32[6,4096]{1,0:T(8,128)S(1)}, s32[6,4096]{1,0:T(8,128)}, u32[]{:S(2)}) copy-start(s32[6,4096]{1,0:T(8,128)} %param.13) | copy-start | bytes 294916
  6.4 30.7 %all-to-all-start.1 = ((f32[8,200,128]{2,1,0:T(8,128)}), f32[8,200,128]{2,1,0:T(8,128)S(1)}, u32[]{:S(2)}, u32[]{:S(2)}) async-start(f32[8,200,128]{2,1,0:T(8,128)} %pad_maximum_fusion), calls=%async_computation.1 | async-start | bytes 1638400 | tf_op jit(solution)/shard_map/all_to_all | solution.py:289
  10.9 1.0 copy-start.2
  26.8 0.6 copy-start.5
  27.4 0.6 copy-start.6
  37.1 25.0 %all-to-all-start = ((f32[4,3,16,1024]{3,2,1,0:T(8,128)}), f32[4,3,16,1024]{3,2,1,0:T(8,128)S(1)}, u32[]{:S(2)}, u32[]{:S(2)}) async-start(f32[4,3,16,1024]{3,2,1,0:T(8,128)} %shard_map.111), calls=%async_computation | async-start | bytes 1572864 | tf_op jit(solution)/shard_map/all_to_all | solution.py:313
  62.1 0.9 copy-start
  102.6 15.2 %collective-permute-start.2 = (f32[16,1024]{1,0:T(8,128)}, f32[16,1024]{1,0:T(8,128)S(1)}, u32[]{:S(2)}, u32[]{:S(2)}) collective-permute-start(f32[16,1024]{1,0:T(8,128)} %get-tuple-element.15), channel_id=1, source_target_pairs={{0,4},{4,8},{8,12},{12,16},{16,20},{20,24},{24,28},{28,0},{1,5},{5... | collective-permute-start | bytes 196616 | tf_op jit(solution)/shard_map/ppermute | solution.py:336
  105.7 12.2 %collective-permute-start.3 = (f32[16,1024]{1,0:T(8,128)}, f32[16,1024]{1,0:T(8,128)S(1)}, u32[]{:S(2)}, u32[]{:S(2)}) collective-permute-start(f32[16,1024]{1,0:T(8,128)} %get-tuple-element.16), channel_id=1, source_target_pairs={{4,0},{8,4},{12,8},{16,12},{20,16},{24,20},{28,24},{0,28},{5,1},{9... | collective-permute-start | bytes 196616 | tf_op jit(solution)/shard_map/ppermute | solution.py:335
  117.9 0.6 copy-start.7
  118.5 0.6 copy-start.8

commit v2 on v1

--- a/solution.py
+++ b/solution.py
@@ -90,82 +90,91 @@
             out_ref[:, start : start + width] = pick(tiles, ids, iota, rows, 0)
 
 
-def curl_kernel(*refs, width, first, sources, added):
-    source_refs = refs[:sources]
-    ids_ref, curl_ref = refs[sources : sources + 2]
-    prior_ref = refs[sources + 2] if added else None
-    out_ref, tiles = refs[-2:]
+def element_rows(ref, index, chunk, width, block, span, owners):
+    step = min(width, span)
+    rows = []
+    for part in range(width // step):
+        place = chunk * width + part * step
+        column = (place // span * owners + block) * span + place % span
+        rows.append(ref[(*index, pl.ds(pl.multiple_of(column, step), step))])
+    return rows[0] if len(rows) == 1 else jnp.concatenate(rows, axis=1)
+
+
+def curl_kernel(block_ref, *refs, width, span, owners):
+    source_refs, (ids_ref, curl_ref, out_ref, tiles) = refs[:-4], refs[-4:]
     rows = source_refs[0].shape[0]
     start = 0
     for source_ref in source_refs:
         size = source_ref.shape[1] // WIDE * rows
         fill_tiles(source_ref, tiles.at[start : start + size])
         start += size
-    blocks, nodes, length = ids_ref.shape
-    steps = length // width
+    block = block_ref[0]
+    nodes = ids_ref.shape[0]
     iota = lax.broadcasted_iota(jnp.int32, (WIDE, width), 0)
 
-    def body(step, carry):
-        block = step // steps
-        column = pl.multiple_of(step % steps * width, width)
-        window = pl.ds(column, width)
-        sums = [prior_ref[block, i, :, window] if added else None for i in range(3)]
+    def body(chunk, carry):
+        take = functools.partial(
+            element_rows, chunk=chunk, width=width, block=block, span=span, owners=owners
+        )
+        sums = [None] * 3
         for j in range(nodes):
-            found = pick(tiles, ids_ref[block, pl.ds(j, 1), window], iota, rows, first)
+            found = pick(tiles, take(ids_ref, (pl.ds(j, 1),)), iota, rows, 0)
             for i in range(3):
-                weight = jnp.broadcast_to(curl_ref[block, i, pl.ds(j, 1), window], found.shape)
+                weight = jnp.broadcast_to(take(curl_ref, (i, pl.ds(j, 1))), found.shape)
                 sums[i] = weight * found if sums[i] is None else sums[i] + weight * found
         for i in range(3):
-            out_ref[block, i, :, window] = sums[i]
+            out_ref[i, :, pl.ds(pl.multiple_of(chunk * width, width), width)] = sums[i]
         return carry
 
-    lax.fori_loop(0, blocks * steps, body, 0)
-
-
-def curls(sources, ids, curl, first, prior=None):
+    lax.fori_loop(0, out_ref.shape[2] // width, body, 0)
+
+
+def curls(block, sources, ids, curl, span, owners):
     rows = sources[0].shape[0]
-    blocks, nodes, length = ids.shape
+    length = ids.shape[1] // owners
     width = min(512, length)
     tiles = sum(s.shape[1] for s in sources) // WIDE
-    extra = () if prior is None else (prior,)
     return pl.pallas_call(
-        functools.partial(
-            curl_kernel, width=width, first=first, sources=len(sources), added=prior is not None
-        ),
-        out_shape=jax.ShapeDtypeStruct((blocks, 3, rows, length), F32),
-        in_specs=[VM] * (len(sources) + 2 + len(extra)),
+        functools.partial(curl_kernel, width=width, span=span, owners=owners),
+        out_shape=jax.ShapeDtypeStruct((3, rows, length), F32),
+        in_specs=[SM] + [VM] * (len(sources) + 2),
         out_specs=VM,
         scratch_shapes=[pltpu.VMEM((tiles * rows, 2 * WIDE), BF)],
-        cost_estimate=cost(tiles * rows * WIDE * 4 * blocks * nodes * length),
-    )(*sources, ids, curl, *extra)
-
-
-def assemble_kernel(field_ref, ids_ref, curl_ref, *refs, width, first, counts):
-    out_refs, sums = refs[:-1], refs[-1]
-    blocks, _, rows, length = field_ref.shape
-    nodes = ids_ref.shape[1]
-    steps = length // width
-    count = sum(counts)
-    sums[...] = jnp.zeros_like(sums)
+        cost_estimate=cost(tiles * rows * WIDE * 4 * ids.shape[0] * length),
+    )(block, *sources, ids, curl)
+
+
+def assemble_kernel(block_ref, field_ref, ids_ref, curl_ref, *refs, width, span, owners, first, counts, added):
+    prior_ref = refs[0] if added else None
+    out_refs, sums = refs[1 if added else 0 : -1], refs[-1]
+    _, rows, length = field_ref.shape
+    block = block_ref[0]
+    nodes = ids_ref.shape[0]
+    count = sums.shape[0] // rows
+    sums[...] = prior_ref[first * rows : (first + count) * rows, :] if added else jnp.zeros_like(sums)
     iota = lax.broadcasted_iota(jnp.int32, (WIDE, width), 0)
 
-    def body(step, carry):
-        block = step // steps
-        column = pl.multiple_of(step % steps * width, width)
-        window = pl.ds(column, width)
-        field = [field_ref[block, i, :, window] for i in range(3)]
+    def body(chunk, carry):
+        take = functools.partial(
+            element_rows, chunk=chunk, width=width, block=block, span=span, owners=owners
+        )
+        window = pl.ds(pl.multiple_of(chunk * width, width), width)
+        field = [field_ref[i, :, window] for i in range(3)]
         total = None
         for j in range(nodes):
             value = None
             for i in range(3):
-                weight = jnp.broadcast_to(curl_ref[block, i, pl.ds(j, 1), window], field[i].shape)
+                weight = jnp.broadcast_to(take(curl_ref, (i, pl.ds(j, 1))), field[i].shape)
                 value = weight * field[i] if value is None else value + weight * field[i]
-            term = spread(value, ids_ref[block, pl.ds(j, 1), window], iota, first, count)
+            term = spread(value, take(ids_ref, (pl.ds(j, 1),)), iota, first, count)
             total = term if total is None else total + term
         sums[...] += total
         return carry
 
-    lax.fori_loop(0, blocks * steps, body, 0)
+    lax.fori_loop(0, length // width, body, 0)
+    if counts is None:
+        out_refs[0][...] = sums[...]
+        return
     tile = 0
     for out_ref, number in zip(out_refs, counts):
         for part in range(number):
@@ -173,18 +182,25 @@
             tile += 1
 
 
-def assemble(field, ids, curl, first, counts):
-    blocks, _, rows, length = field.shape
+def assemble(block, field, ids, curl, span, owners, prior, first, count, counts=None):
+    _, rows, length = field.shape
     width = min(512, length)
-    tiles = sum(counts)
+    extra = () if prior is None else (prior,)
+    if counts is None:
+        out_shape = [jax.ShapeDtypeStruct((count * rows, WIDE), F32)]
+    else:
+        out_shape = [jax.ShapeDtypeStruct((rows, n * WIDE), F32) for n in counts]
     return pl.pallas_call(
-        functools.partial(assemble_kernel, width=width, first=first, counts=counts),
-        out_shape=[jax.ShapeDtypeStruct((rows, n * WIDE), F32) for n in counts],
-        in_specs=[VM] * 3,
-        out_specs=[VM] * len(counts),
-        scratch_shapes=[pltpu.VMEM((tiles * rows, WIDE), F32)],
-        cost_estimate=cost(tiles * rows * WIDE * 4 * blocks * ids.shape[1] * length),
-    )(field, ids, curl)
+        functools.partial(
+            assemble_kernel, width=width, span=span, owners=owners, first=first, counts=counts,
+            added=prior is not None,
+        ),
+        out_shape=out_shape,
+        in_specs=[SM] + [VM] * (3 + len(extra)),
+        out_specs=[VM] * len(out_shape),
+        scratch_shapes=[pltpu.VMEM((count * rows, WIDE), F32)],
+        cost_estimate=cost(count * rows * WIDE * 4 * ids.shape[0] * length),
+    )(block, field, ids, curl, *extra)
 
 
 def finish_kernel(own_ref, below_ref, above_ref, faces_ref, out_ref, *, width):
@@ -238,9 +254,14 @@
     lax.fori_loop(0, samples // 8, body, 0)
 
 
-def tensor_kernel(flux_ref, point_ref, nu_ref, twice_ref, inverse_ref, forward_ref, out_ref):
-    blocks, _, rows, length = flux_ref.shape
+def tensor_kernel(me_ref, *refs):
+    blocks = (len(refs) - 5) // 2
+    flux_refs, out_refs = refs[:blocks], refs[blocks + 5 :]
+    point_ref, nu_ref, twice_ref, inverse_ref, forward_ref = refs[blocks : blocks + 5]
+    _, rows, length = flux_refs[0].shape
     samples = blocks * rows
+    me = me_ref[0]
+    inverse, forward = inverse_ref[me], forward_ref[me]
     dot = functools.partial(
         jnp.dot, precision=lax.Precision.HIGHEST, preferred_element_type=F32
     )
@@ -250,15 +271,28 @@
         b = [point_ref[i * samples : (i + 1) * samples, window] for i in range(3)]
         flux = []
         for i in range(3):
-            packed = jnp.concatenate([flux_ref[k, i, :, window] for k in range(blocks)], axis=0)
-            flux.append(dot(inverse_ref[...], packed))
+            packed = jnp.concatenate([ref[i, :, window] for ref in flux_refs], axis=0)
+            flux.append(dot(inverse, packed))
         along = b[0] * flux[0] + b[1] * flux[1] + b[2] * flux[2]
         along = along * twice_ref[:, window]
         nu = nu_ref[:, window]
         for i in range(3):
-            coefs = dot(forward_ref[...], nu * flux[i] + along * b[i])
-            for k in range(blocks):
-                out_ref[k, i, :, window] = coefs[k * rows : (k + 1) * rows]
+            coefs = dot(forward, nu * flux[i] + along * b[i])
+            for k, ref in enumerate(out_refs):
+                ref[i, :, window] = coefs[k * rows : (k + 1) * rows]
+
+
+def ordered_tables(samples, owners):
+    inverse, forward = dft_tables(samples)
+    rows = samples // owners
+    inverse = inverse.reshape(samples, owners, rows)
+    forward = forward.reshape(owners, rows, samples)
+    arrival = [[(me - k) % owners for k in range(owners)] for me in range(owners)]
+    sending = [[(me + k) % owners for k in range(owners)] for me in range(owners)]
+    return (
+        np.stack([inverse[:, o].reshape(samples, samples) for o in arrival]),
+        np.stack([forward[o].reshape(samples, samples) for o in sending]),
+    )
 
 
 def per_device(
@@ -289,10 +323,19 @@
     points = lax.all_to_all(points, "mesh", split_axis=0, concat_axis=0, tiled=True)
     points = jnp.transpose(points, (1, 0, 2)).reshape(3 * samples + 8, length)
 
-    ids = connectivity.reshape(nodes, mesh_count, harm_count, block)
-    ids = jnp.transpose(ids, (2, 0, 1, 3)).reshape(harm_count, nodes, length)
-    curl = curl_vectors.reshape(3, nodes, mesh_count, harm_count, block)
-    curl = jnp.transpose(curl, (3, 0, 1, 2, 4)).reshape(harm_count, 3, nodes, length)
+    ids, curl, span = connectivity, curl_vectors, block
+    if block % 128:
+        span = length
+        ids = ids.reshape(nodes, mesh_count, harm_count, block)
+        ids = jnp.transpose(ids, (0, 2, 1, 3)).reshape(nodes, elements)
+        curl = curl.reshape(3, nodes, mesh_count, harm_count, block)
+        curl = jnp.transpose(curl, (0, 1, 3, 2, 4)).reshape(3, nodes, elements)
+    me = lax.axis_index("harm")
+    at = [jnp.reshape((me + k) % harm_count, (1,)) for k in range(harm_count)]
+    order = sorted(range(1, harm_count), key=lambda k: (-min(k, harm_count - k), k))
+
+    def send(value, k):
+        return lax.ppermute(value, "harm", [(i, (i + k) % harm_count) for i in range(harm_count)])
 
     face_width = min(512, face_len)
     own_tiles, face_tiles = own // WIDE, face_len // WIDE
@@ -308,9 +351,10 @@
     before = lax.ppermute(upper, "mesh", up)
     after = lax.ppermute(lower, "mesh", down)
 
-    partial = curls([field_in], ids, curl, 0)
-    flux = curls([before, after], ids, curl, own_tiles, partial)
-    flux = lax.all_to_all(flux, "harm", split_axis=0, concat_axis=0, tiled=True)
+    flux = {}
+    for k in order + [0]:
+        piece = curls(at[k], [field_in, before, after], ids, curl, span, harm_count)
+        flux[k] = send(piece, k) if k else piece
 
     plane = jax.ShapeDtypeStruct((samples, length), F32)
     nu, twice = pl.pallas_call(
@@ -321,20 +365,35 @@
         cost_estimate=cost(samples * length * 8 * 40),
     )(bh_knots, curve_base, curve_slopes, points)
 
-    inverse, forward = dft_tables(samples)
-    field = pl.pallas_call(
+    inverse, forward = ordered_tables(samples, harm_count)
+    piece = jax.ShapeDtypeStruct((3, rows, length), F32)
+    fields = pl.pallas_call(
         tensor_kernel,
-        out_shape=jax.ShapeDtypeStruct(flux.shape, F32),
-        in_specs=[VM] * 6,
-        out_specs=VM,
+        out_shape=[piece] * harm_count,
+        in_specs=[SM] + [VM] * (harm_count + 5),
+        out_specs=[VM] * harm_count,
         cost_estimate=cost(samples * samples * length * 6 * 12),
-    )(flux, points, nu, twice, inverse, forward)
-    field = lax.all_to_all(field, "harm", split_axis=0, concat_axis=0, tiled=True)
-
-    low_sums, high_sums = assemble(field, ids, curl, own_tiles, (face_tiles, face_tiles))
+    )(at[0], *(flux[k] for k in range(harm_count)), points, nu, twice, inverse, forward)
+
+    back = order[::-1]
+    field = {k: send(fields[k], k) for k in back}
+    field[0] = fields[0]
+    put = functools.partial(assemble, ids=ids, curl=curl, span=span, owners=harm_count)
+    tiles = own_tiles + 2 * face_tiles
+    sums = None
+    for k in [0] + back[:-1]:
+        (sums,) = put(at[-k % harm_count], field[k], prior=sums, first=0, count=tiles)
+    last = back[-1]
+    where = at[-last % harm_count]
+    low_sums, high_sums = put(
+        where, field[last], prior=sums, first=own_tiles, count=2 * face_tiles,
+        counts=(face_tiles, face_tiles),
+    )
     above = lax.ppermute(low_sums, "mesh", down)
     below = lax.ppermute(high_sums, "mesh", up)
-    (own_sums,) = assemble(field, ids, curl, 0, (own_tiles,))
+    (own_sums,) = put(
+        where, field[last], prior=sums, first=0, count=own_tiles, counts=(own_tiles,)
+    )
     return pl.pallas_call(
         functools.partial(finish_kernel, width=face_width),
         out_shape=jax.ShapeDtypeStruct((rows, own), F32),

time: 124 us -> 96.9 us (0.78)
  the two profiles are of different devices: /device:TPU:1 before, /device:TPU:12 now
where the time goes in v2:
time: 96.9 us; the launch traced here: 96.4 us
  Pallas kernels  61.2 us (63%)
  starting transfers between devices  16.7 us (17%)
  waiting for transfers between devices  11.6 us (12%)
  local copies, waits for them, and re-layouts  5.85 us (6%)
    pallas_call x5, Pallas kernels, assemble(): pl.pallas_call(functools.partial(assemble_kernel, width=width, span=span,...  25.4 us
    pallas_call x4, Pallas kernels, curls(): pl.pallas_call(functools.partial(curl_kernel, width=width, span=span, own...  21.9 us
    ppermute x6, waiting for transfers between devices, send(): lax.ppermute(value, 'harm', [(i, (i + k) % harm_count) for i in range(har...  11.6 us
    ppermute x6, starting transfers between devices, send(): lax.ppermute(value, 'harm', [(i, (i + k) % harm_count) for i in range(har...  7.42 us
    unnamed x25, local copies, waits for them, and re-layouts  4.84 us
    pallas_call x1, Pallas kernels, per_device(): pl.pallas_call(tensor_kernel, out_shape=[piece] * harm_count, in_specs=[S...  4.68 us
    all_to_all x1, starting transfers between devices, per_device(): lax.all_to_all(points, 'mesh', split_axis=0, concat_axis=0, tiled=True)  3.98 us
    pallas_call x1, Pallas kernels, per_device(): pl.pallas_call(curve_kernel, out_shape=[plane, plane], in_specs=[SM] * 3...  3.95 us
  transfers between devices with their start and end apart: 11, of which 1 were waited for; matrix products, arithmetic and copies ran while one was open for 2% of the time, Pallas kernels for 49%

profile of v2, /device:TPU:12, one launch (start us, length us, event | category | flops | bytes accessed | tf_op | source)
XLA Modules:
  0.0 96.4 jit_solution(15943560413194103334)
XLA Ops:
  0.0 2.7 %shard_map.109 = (f32[16,1024]{1,0:T(8,128)}, f32[16,1024]{1,0:T(8,128)}) custom-call(f32[16,5120]{1,0:T(8,128)} %refs_0_.7, s32[2,1024]{1,0:T(2,128)} %faces_ref.3), custom_call_target="tpu_custom_call" | custom-call | flops 671088640 | bytes 4194304 | tf_op jit(solution)/shard_map/pallas_call | solution.py:343
  2.7 2.6 %collective-permute-start.1 = (f32[16,1024]{1,0:T(8,128)}, f32[16,1024]{1,0:T(8,128)S(1)}, u32[]{:S(2)}, u32[]{:S(2)}) collective-permute-start(f32[16,1024]{1,0:T(8,128)} %get-tuple-element.16), channel_id=1, source_target_pairs={{4,0},{8,4},{12,8},{16,12},{20,16},{24,20},{28,24},{0,28},{5,1},{9... | collective-permute-start | bytes 196616 | tf_op jit(solution)/shard_map/ppermute | solution.py:352
  5.5 1.0 pad_maximum_fusion
  6.5 4.0 %all-to-all-start = ((f32[8,200,128]{2,1,0:T(8,128)}), f32[8,200,128]{2,1,0:T(8,128)S(1)}, u32[]{:S(2)}, u32[]{:S(2)}) async-start(f32[8,200,128]{2,1,0:T(8,128)} %pad_maximum_fusion), calls=%async_computation | async-start | bytes 1638400 | tf_op jit(solution)/shard_map/all_to_all | solution.py:323
  11.1 5.5 %shard_map.111 = f32[3,16,1024]{2,1,0:T(8,128)} custom-call(s32[1]{0:T(128)} %bitcast.2.block_ref, f32[16,5120]{1,0:T(8,128)} %refs_0_.7, f32[16,1024]{1,0:T(8,128)} %copy-done.8, f32[16,1024]{1,0:T(8,128)} %copy-done.9, s32[6,4096]{1,0:T(8,128)} %ids_ref.9, f32[3,6,4096]{2,1,0:T(8,128)} %curl_ref.9), custom_call_target="tpu_custom_call" | custom-call | flops 2818572288 | bytes 4194304 | tf_op jit(solution)/shard_map/pallas_call | solution.py:137
  16.6 1.6 %collective-permute-start.2 = (f32[3,16,1024]{2,1,0:T(8,128)}, f32[3,16,1024]{2,1,0:T(8,128)S(1)}, u32[]{:S(2)}, u32[]{:S(2)}) collective-permute-start(f32[3,16,1024]{2,1,0:T(8,128)} %shard_map.111), channel_id=1, source_target_pairs={{0,1},{1,2},{2,3},{3,0},{4,5},{5,6},{6,7},{7,4},{8,9},{9,10},{10,1... | collective-permute-start | bytes 589832 | tf_op jit(solution)/shard_map/ppermute | solution.py:338
  18.2 5.5 %shard_map.112 = f32[3,16,1024]{2,1,0:T(8,128)} custom-call(s32[1]{0:T(128)} %bitcast.block_ref, f32[16,5120]{1,0:T(8,128)} %refs_0_.7, f32[16,1024]{1,0:T(8,128)} %copy-done.8, f32[16,1024]{1,0:T(8,128)} %copy-done.9, s32[6,4096]{1,0:T(8,128)} %ids_ref.9, f32[3,6,4096]{2,1,0:T(8,128)} %curl_ref.9), custom_call_target="tpu_custom_call" | custom-call | flops 2818572288 | bytes 4194304 | tf_op jit(solution)/shard_map/pallas_call | solution.py:137
  23.6 1.0 %collective-permute-start.3 = (f32[3,16,1024]{2,1,0:T(8,128)}, f32[3,16,1024]{2,1,0:T(8,128)S(1)}, u32[]{:S(2)}, u32[]{:S(2)}) collective-permute-start(f32[3,16,1024]{2,1,0:T(8,128)} %shard_map.112), channel_id=1, source_target_pairs={{0,2},{1,3},{2,0},{3,1},{4,6},{5,7},{6,4},{7,5},{8,10},{9,11},{10,... | collective-permute-start | bytes 589832 | tf_op jit(solution)/shard_map/ppermute | solution.py:338
  24.6 5.5 %shard_map.113 = f32[3,16,1024]{2,1,0:T(8,128)} custom-call(s32[1]{0:T(128)} %bitcast.3.block_ref, f32[16,5120]{1,0:T(8,128)} %refs_0_.7, f32[16,1024]{1,0:T(8,128)} %copy-done.8, f32[16,1024]{1,0:T(8,128)} %copy-done.9, s32[6,4096]{1,0:T(8,128)} %ids_ref.9, f32[3,6,4096]{2,1,0:T(8,128)} %curl_ref.9), custom_call_target="tpu_custom_call" | custom-call | flops 2818572288 | bytes 4194304 | tf_op jit(solution)/shard_map/pallas_call | solution.py:137
  30.1 2.0 %collective-permute-start.4 = (f32[3,16,1024]{2,1,0:T(8,128)}, f32[3,16,1024]{2,1,0:T(8,128)S(1)}, u32[]{:S(2)}, u32[]{:S(2)}) collective-permute-start(f32[3,16,1024]{2,1,0:T(8,128)} %shard_map.113), channel_id=1, source_target_pairs={{0,3},{1,0},{2,1},{3,2},{4,7},{5,4},{6,5},{7,6},{8,11},{9,8},{10,9... | collective-permute-start | bytes 589832 | tf_op jit(solution)/shard_map/ppermute | solution.py:338
  32.1 5.5 %shard_map.110.refs_0_ = f32[3,16,1024]{2,1,0:T(8,128)} custom-call(s32[1]{0:T(128)} %bitcast.1.block_ref.me_ref, f32[16,5120]{1,0:T(8,128)} %refs_0_.7, f32[16,1024]{1,0:T(8,128)} %copy-done.8, f32[16,1024]{1,0:T(8,128)} %copy-done.9, s32[6,4096]{1,0:T(8,128)} %ids_ref.9, f32[3,6,4096]{2,1,0:T(8,128)} %curl_ref.9), custom_call_target="tpu_custom_call" | custom-call | flops 2818572288 | bytes 4194304 | tf_op jit(solution)/shard_map/pallas_call | solution.py:137
  37.6 1.0 %copy_bitcast_fusion.point_ref.refs_4_ = f32[200,1024]{1,0:T(8,128)} fusion(f32[8,200,128]{2,1,0:T(8,128)S(1)} %all-to-all-done), kind=kLoop, calls=%fused_computation | loop fusion | bytes 1638400 | tf_op jit(solution)/shard_map/reshape | solution.py:324
  38.6 3.9 %shard_map.114 = (f32[64,1024]{1,0:T(8,128)}, f32[64,1024]{1,0:T(8,128)}) custom-call(s32[8]{0:T(128)} %knots_ref.1, f32[4]{0:T(128)} %base_ref.1, f32[4,8]{1,0:T(4,128)} %slopes_ref.1, f32[200,1024]{1,0:T(8,128)} %copy_bitcast_fusion.point_ref.refs_4_), custom_call_target="tpu_custom_call" | custom-call | flops 20971520 | bytes 4194304 | tf_op jit(solution)/shard_map/pallas_call | solution.py:360
  43.4 4.7 %shard_map.115 = (f32[3,16,1024]{2,1,0:T(8,128)}, f32[3,16,1024]{2,1,0:T(8,128)}, f32[3,16,1024]{2,1,0:T(8,128)}, f32[3,16,1024]{2,1,0:T(8,128)}) custom-call(s32[1]{0:T(128)} %bitcast.1.block_ref.me_ref, f32[3,16,1024]{2,1,0:T(8,128)} %shard_map.110.refs_0_, f32[3,16,1024]{2,1,0:T(8,128)} %copy-done.1, f32[3,16,1024]{2,1,0:T(8,128)} %copy-done.2, ...), custom_call_target="tpu_custom_call" | custom-call | flops 301989888 | bytes 4194304 | tf_op jit(solution)/shard_map/pallas_call | solution.py:370
  48.4 2.5 %collective-permute-start.6 = (f32[3,16,1024]{2,1,0:T(8,128)}, f32[3,16,1024]{2,1,0:T(8,128)S(1)}, u32[]{:S(2)}, u32[]{:S(2)}) collective-permute-start(f32[3,16,1024]{2,1,0:T(8,128)} %get-tuple-element.20), channel_id=1, source_target_pairs={{0,1},{1,2},{2,3},{3,0},{4,5},{5,6},{6,7},{7,4},{8,9},{9,10},{10,1... | collective-permute-start | bytes 589832 | tf_op jit(solution)/shard_map/ppermute | solution.py:338
  50.9 5.4 %shard_map.116.refs_0_ = f32[448,256]{1,0:T(8,128)} custom-call(s32[1]{0:T(128)} %bitcast.1.block_ref.me_ref, f32[3,16,1024]{2,1,0:T(8,128)} %get-tuple-element.22.field_ref, s32[6,4096]{1,0:T(8,128)} %ids_ref.9, f32[3,6,4096]{2,1,0:T(8,128)} %curl_ref.9), custom_call_target="tpu_custom_call" | custom-call | flops 2818572288 | bytes 4194304 | tf_op jit(solution)/shard_map/pallas_call | solution.py:193
  56.2 11.6 %collective-permute-done.7.field_ref = f32[3,16,1024]{2,1,0:T(8,128)S(1)} collective-permute-done((f32[3,16,1024]{2,1,0:T(8,128)}, f32[3,16,1024]{2,1,0:T(8,128)S(1)}, u32[]{:S(2)}, u32[]{:S(2)}) %collective-permute-start.7) | collective-permute-done | bytes 196640 | tf_op jit(solution)/shard_map/ppermute | solution.py:338
  68.5 5.5 %shard_map.117.refs_0_ = f32[448,256]{1,0:T(8,128)} custom-call(s32[1]{0:T(128)} %bitcast.2.block_ref, f32[3,16,1024]{2,1,0:T(8,128)} %copy-done.7, s32[6,4096]{1,0:T(8,128)} %ids_ref.9, f32[3,6,4096]{2,1,0:T(8,128)} %curl_ref.9, f32[448,256]{1,0:T(8,128)} %shard_map.116.refs_0_), custom_call_target="tpu_custom_call" | custom-call | flops 2818572288 | bytes 4194304 | tf_op jit(solution)/shard_map/pallas_call | solution.py:193
  74.0 0.7 copy-done.6
  74.7 5.5 %shard_map.118.refs_0_ = f32[448,256]{1,0:T(8,128)} custom-call(s32[1]{0:T(128)} %bitcast.3.block_ref, f32[3,16,1024]{2,1,0:T(8,128)} %copy-done.6, s32[6,4096]{1,0:T(8,128)} %ids_ref.9, f32[3,6,4096]{2,1,0:T(8,128)} %curl_ref.9, f32[448,256]{1,0:T(8,128)} %shard_map.117.refs_0_), custom_call_target="tpu_custom_call" | custom-call | flops 2818572288 | bytes 4194304 | tf_op jit(solution)/shard_map/pallas_call | solution.py:193
  80.9 4.4 %shard_map.120 = (f32[16,1024]{1,0:T(8,128)}, f32[16,1024]{1,0:T(8,128)}) custom-call(s32[1]{0:T(128)} %bitcast.block_ref, f32[3,16,1024]{2,1,0:T(8,128)} %copy-done.5, s32[6,4096]{1,0:T(8,128)} %ids_ref.9, f32[3,6,4096]{2,1,0:T(8,128)} %curl_ref.9, f32[448,256]{1,0:T(8,128)} %shard_map.118.refs_0_), custom_call_target="tpu_custom_call" | custom-call | flops 805306368 | bytes 4194304 | tf_op jit(solution)/shard_map/pallas_call | solution.py:193
  85.3 2.6 %collective-permute-start.9 = (f32[16,1024]{1,0:T(8,128)}, f32[16,1024]{1,0:T(8,128)S(1)}, u32[]{:S(2)}, u32[]{:S(2)}) collective-permute-start(f32[16,1024]{1,0:T(8,128)} %get-tuple-element.24), channel_id=1, source_target_pairs={{4,0},{8,4},{12,8},{16,12},{20,16},{24,20},{28,24},{0,28},{5,1},{9... | collective-permute-start | bytes 196616 | tf_op jit(solution)/shard_map/ppermute | solution.py:392
  87.9 4.6 %shard_map.119.own_ref = f32[16,5120]{1,0:T(8,128)} custom-call(s32[1]{0:T(128)} %bitcast.block_ref, f32[3,16,1024]{2,1,0:T(8,128)} %copy-done.5, s32[6,4096]{1,0:T(8,128)} %ids_ref.9, f32[3,6,4096]{2,1,0:T(8,128)} %curl_ref.9, f32[448,256]{1,0:T(8,128)} %shard_map.118.refs_0_), custom_call_target="tpu_custom_call" | custom-call | flops 2013265920 | bytes 4194304 | tf_op jit(solution)/shard_map/pallas_call | solution.py:193
  93.8 2.6 %shard_map.121 = f32[16,5120]{1,0:T(8,128)} custom-call(f32[16,5120]{1,0:T(8,128)} %shard_map.119.own_ref, f32[16,1024]{1,0:T(8,128)} %copy-done.10, f32[16,1024]{1,0:T(8,128)} %copy-done.11, s32[2,1024]{1,0:T(2,128)} %faces_ref.3), custom_call_target="tpu_custom_call" | custom-call | flops 671088640 | bytes 4194304 | tf_op jit(solution)/shard_map/pallas_call | solution.py:397
  (40 shorter events, 4.5 us)
Async XLA Ops:
  0.0 5.3 %copy-start = (f32[64,3,8,128]{3,2,1,0:T(8,128)S(1)}, f32[64,3,8,128]{3,2,1,0:T(8,128)}, u32[]{:S(2)}) copy-start(f32[64,3,8,128]{3,2,1,0:T(8,128)} %param.15) | copy-start | bytes 2359300
  0.0 5.3 %copy-start.4 = (s32[8,128]{1,0:T(8,128)S(1)}, s32[8,128]{1,0:T(8,128)}, u32[]{:S(2)}) copy-start(s32[8,128]{1,0:T(8,128)} %param.16) | copy-start | bytes 12292
  2.7 7.8 %collective-permute-start = (f32[16,1024]{1,0:T(8,128)}, f32[16,1024]{1,0:T(8,128)S(1)}, u32[]{:S(2)}, u32[]{:S(2)}) collective-permute-start(f32[16,1024]{1,0:T(8,128)} %get-tuple-element.15), channel_id=1, source_target_pairs={{0,4},{4,8},{8,12},{12,16},{16,20},{20,24},{24,28},{28,0},{1,5},{5... | collective-permute-start | bytes 196616 | tf_op jit(solution)/shard_map/ppermute | solution.py:351
  2.7 7.8 %collective-permute-start.1 = (f32[16,1024]{1,0:T(8,128)}, f32[16,1024]{1,0:T(8,128)S(1)}, u32[]{:S(2)}, u32[]{:S(2)}) collective-permute-start(f32[16,1024]{1,0:T(8,128)} %get-tuple-element.16), channel_id=1, source_target_pairs={{4,0},{8,4},{12,8},{16,12},{20,16},{24,20},{28,24},{0,28},{5,1},{9... | collective-permute-start | bytes 196616 | tf_op jit(solution)/shard_map/ppermute | solution.py:352
  6.5 31.1 %all-to-all-start = ((f32[8,200,128]{2,1,0:T(8,128)}), f32[8,200,128]{2,1,0:T(8,128)S(1)}, u32[]{:S(2)}, u32[]{:S(2)}) async-start(f32[8,200,128]{2,1,0:T(8,128)} %pad_maximum_fusion), calls=%async_computation | async-start | bytes 1638400 | tf_op jit(solution)/shard_map/all_to_all | solution.py:323
  10.4 0.6 copy-start.8
  10.5 0.6 copy-start.9
  16.6 26.0 %collective-permute-start.2 = (f32[3,16,1024]{2,1,0:T(8,128)}, f32[3,16,1024]{2,1,0:T(8,128)S(1)}, u32[]{:S(2)}, u32[]{:S(2)}) collective-permute-start(f32[3,16,1024]{2,1,0:T(8,128)} %shard_map.111), channel_id=1, source_target_pairs={{0,1},{1,2},{2,3},{3,0},{4,5},{5,6},{6,7},{7,4},{8,9},{9,10},{10,1... | collective-permute-start | bytes 589832 | tf_op jit(solution)/shard_map/ppermute | solution.py:338
  23.6 18.9 %collective-permute-start.3 = (f32[3,16,1024]{2,1,0:T(8,128)}, f32[3,16,1024]{2,1,0:T(8,128)S(1)}, u32[]{:S(2)}, u32[]{:S(2)}) collective-permute-start(f32[3,16,1024]{2,1,0:T(8,128)} %shard_map.112), channel_id=1, source_target_pairs={{0,2},{1,3},{2,0},{3,1},{4,6},{5,7},{6,4},{7,5},{8,10},{9,11},{10,... | collective-permute-start | bytes 589832 | tf_op jit(solution)/shard_map/ppermute | solution.py:338
  30.1 12.5 %collective-permute-start.4 = (f32[3,16,1024]{2,1,0:T(8,128)}, f32[3,16,1024]{2,1,0:T(8,128)S(1)}, u32[]{:S(2)}, u32[]{:S(2)}) collective-permute-start(f32[3,16,1024]{2,1,0:T(8,128)} %shard_map.113), channel_id=1, source_target_pairs={{0,3},{1,0},{2,1},{3,2},{4,7},{5,4},{6,5},{7,6},{8,11},{9,8},{10,9... | collective-permute-start | bytes 589832 | tf_op jit(solution)/shard_map/ppermute | solution.py:338
  42.5 0.7 copy-start.1
  42.5 0.7 copy-start.2
  42.6 0.8 copy-start.3
  48.0 32.1 %collective-permute-start.5 = (f32[3,16,1024]{2,1,0:T(8,128)}, f32[3,16,1024]{2,1,0:T(8,128)S(1)}, u32[]{:S(2)}, u32[]{:S(2)}) collective-permute-start(f32[3,16,1024]{2,1,0:T(8,128)} %get-tuple-element.19), channel_id=1, source_target_pairs={{0,2},{1,3},{2,0},{3,1},{4,6},{5,7},{6,4},{7,5},{8,10},{9,11},{10,... | collective-permute-start | bytes 589832 | tf_op jit(solution)/shard_map/ppermute | solution.py:338
  48.4 25.6 %collective-permute-start.6 = (f32[3,16,1024]{2,1,0:T(8,128)}, f32[3,16,1024]{2,1,0:T(8,128)S(1)}, u32[]{:S(2)}, u32[]{:S(2)}) collective-permute-start(f32[3,16,1024]{2,1,0:T(8,128)} %get-tuple-element.20), channel_id=1, source_target_pairs={{0,1},{1,2},{2,3},{3,0},{4,5},{5,6},{6,7},{7,4},{8,9},{9,10},{10,1... | collective-permute-start | bytes 589832 | tf_op jit(solution)/shard_map/ppermute | solution.py:338
  50.9 17.0 %collective-permute-start.7 = (f32[3,16,1024]{2,1,0:T(8,128)}, f32[3,16,1024]{2,1,0:T(8,128)S(1)}, u32[]{:S(2)}, u32[]{:S(2)}) collective-permute-start(f32[3,16,1024]{2,1,0:T(8,128)} %get-tuple-element.21), channel_id=1, source_target_pairs={{0,3},{1,0},{2,1},{3,2},{4,7},{5,4},{6,5},{7,6},{8,11},{9,8},{10,9... | collective-permute-start | bytes 589832 | tf_op jit(solution)/shard_map/ppermute | solution.py:338
  67.8 0.7 copy-start.7
  74.0 0.7 copy-start.6
  80.2 0.7 copy-start.5
  85.3 7.3 %collective-permute-start.8 = (f32[16,1024]{1,0:T(8,128)}, f32[16,1024]{1,0:T(8,128)S(1)}, u32[]{:S(2)}, u32[]{:S(2)}) collective-permute-start(f32[16,1024]{1,0:T(8,128)} %get-tuple-element.23), channel_id=1, source_target_pairs={{0,4},{4,8},{8,12},{12,16},{16,20},{20,24},{24,28},{28,0},{1,5},{5... | collective-permute-start | bytes 196616 | tf_op jit(solution)/shard_map/ppermute | solution.py:393
  85.3 7.3 %collective-permute-start.9 = (f32[16,1024]{1,0:T(8,128)}, f32[16,1024]{1,0:T(8,128)S(1)}, u32[]{:S(2)}, u32[]{:S(2)}) collective-permute-start(f32[16,1024]{1,0:T(8,128)} %get-tuple-element.24), channel_id=1, source_target_pairs={{4,0},{8,4},{12,8},{16,12},{20,16},{24,20},{28,24},{0,28},{5,1},{9... | collective-permute-start | bytes 196616 | tf_op jit(solution)/shard_map/ppermute | solution.py:392
  92.6 0.6 copy-start.10
  93.2 0.6 copy-start.11
